TPU v7x, 128 devices: a whole 4x4x4 slice. The times are simulated.
128 devices in a mesh: rep: 16 (over y_hi, z, core), tp: 8 (over y_lo, x).
Axes of the slice: x: 4, y: 4 (y_hi: 2, y_lo: 2; y = y_hi * 2 + y_lo), z: 4, core: 2. Of those that a mesh axis runs over, the one named last changes fastest.
Arguments:
- delta_query: bfloat16 [16, 2, 2048, 3072], P('rep', None, None, 'tp'), may hold values from -6 to 6
- master_query: float32 [2, 2048, 3072], P(None, 'rep', 'tp'), may hold values from -3 to 3
- moment_query: float32 [2, 2048, 3072], P(None, 'rep', 'tp'), may hold values from -3 to 3
- delta_latent: bfloat16 [16, 2, 512, 4096], P('rep', None, None, 'tp'), may hold values from -6 to 6
- master_latent: float32 [2, 512, 4096], P(None, 'rep', 'tp'), may hold values from -3 to 3
- moment_latent: float32 [2, 512, 4096], P(None, 'rep', 'tp'), may hold values from -3 to 3
- delta_output: bfloat16 [16, 2, 2048, 2048], P('rep', None, 'tp'), may hold values from -6 to 6
- master_output: float32 [2, 2048, 2048], P(None, 'tp', 'rep'), may hold values from -3 to 3
- moment_output: float32 [2, 2048, 2048], P(None, 'tp', 'rep'), may hold values from -3 to 3
Outputs:
- params_query: bfloat16 [2, 2048, 3072], P(None, None, 'tp')
- new_master_query: float32 [2, 2048, 3072], P(None, 'rep', 'tp')
- new_moment_query: float32 [2, 2048, 3072], P(None, 'rep', 'tp')
- params_latent: bfloat16 [2, 512, 4096], P(None, None, 'tp')
- new_master_latent: float32 [2, 512, 4096], P(None, 'rep', 'tp')
- new_moment_latent: float32 [2, 512, 4096], P(None, 'rep', 'tp')
- params_output: bfloat16 [2, 2048, 2048], P(None, 'tp')
- new_master_output: float32 [2, 2048, 2048], P(None, 'tp', 'rep')
- new_moment_output: float32 [2, 2048, 2048], P(None, 'tp', 'rep')
All inputs are finite; a program needn't handle non-finite values.
Results may differ from a plain program's by a relative error of at most 0.012.
Values may be sent and summed in bfloat16 or wider, within the bound.
A program may use at most 64 MiB of HBM per device.

v0:
```python
import jax
import jax.numpy as jnp
from jax import lax
from jax.sharding import Mesh
from jax.sharding import PartitionSpec as P

REP = ("rep_0", "rep_1", "rep_2")
OUTER_RATE = 0.7
OUTER_MOMENTUM = 0.9


def in_blocks(value, dim, length):
    lengths = value.shape
    blocks = value.reshape(*lengths[:dim], length, lengths[dim] // length, *lengths[dim + 1 :])
    return jnp.moveaxis(blocks, dim, 0)


def joined_along(blocks, dim):
    lengths = list(blocks.shape[1:])
    lengths[dim] *= blocks.shape[0]
    return jnp.moveaxis(blocks, 0, dim).reshape(lengths)


def moved_by_axis(blocks, axes, order):
    inside = blocks.shape[1:]
    out = blocks.reshape(*(lax.axis_size(a) for a in axes), *inside)
    for k in order:
        out = lax.all_to_all(out, axes[k], k, k, tiled=True)
    return out.reshape(-1, *inside)


def core_and_chips(value, groups, order, split_dim, concat_dim):
    length = lax.axis_size(groups[0]) * lax.axis_size(groups[1])
    blocks = in_blocks(value, split_dim, length)
    return joined_along(moved_by_axis(blocks, groups, order), concat_dim)


def copy_for_each(value, axis):
    length = lax.axis_size(axis)
    return lax.all_to_all(
        jnp.broadcast_to(value[None], (length, *value.shape)), axis, 0, 0, tiled=True
    )


def gathered_copies(value, axis, dim):
    blocks = copy_for_each(value, axis)
    return joined_along(blocks, dim)


def nesterov(totals, master, moment, replica_count):
    average = totals / replica_count
    momentum = OUTER_MOMENTUM * moment + average
    updated = master - OUTER_RATE * (average + OUTER_MOMENTUM * momentum)
    return (updated, momentum)


def outer_step(
    delta_query,
    master_query,
    moment_query,
    delta_latent,
    master_latent,
    moment_latent,
    delta_output,
    master_output,
    moment_output,
):
    replica_count = lax.axis_size(REP)
    query_terms = core_and_chips(delta_query, (("rep_0", "rep_1"), "rep_2"), (1, 0), 2, 0)
    latent_terms = lax.all_to_all(delta_latent, REP, split_axis=2, concat_axis=0, tiled=True)
    output_terms = lax.all_to_all(delta_output, REP, split_axis=3, concat_axis=0, tiled=True)
    query_totals = jnp.sum(query_terms.astype(jnp.float32), 0)
    latent_totals = jnp.sum(latent_terms.astype(jnp.float32), 0)
    output_totals = jnp.sum(output_terms.astype(jnp.float32), 0)
    query_master, query_moment = nesterov(query_totals, master_query, moment_query, replica_count)
    latent_master, latent_moment = nesterov(
        latent_totals, master_latent, moment_latent, replica_count
    )
    output_master, output_moment = nesterov(
        output_totals, master_output, moment_output, replica_count
    )
    query_params = lax.all_gather(query_master.astype(jnp.bfloat16), REP, axis=1, tiled=True)
    latent_params = gathered_copies(latent_master.astype(jnp.bfloat16), REP, 1)
    output_params = lax.all_gather(output_master.astype(jnp.bfloat16), REP, axis=2, tiled=True)
    return (
        query_params,
        query_master,
        query_moment,
        latent_params,
        latent_master,
        latent_moment,
        output_params,
        output_master,
        output_moment,
    )


def on_device(
    delta_query,
    master_query,
    moment_query,
    delta_latent,
    master_latent,
    moment_latent,
    delta_output,
    master_output,
    moment_output,
):
    return outer_step(
        delta_query,
        master_query,
        moment_query,
        delta_latent,
        master_latent,
        moment_latent,
        delta_output,
        master_output,
        moment_output,
    )


def solution(mesh):
    torus = Mesh(mesh.devices.reshape(2, 4, 2, mesh.shape["tp"]), ("rep_0", "rep_1", "rep_2", "tp"))
    return jax.shard_map(
        on_device,
        mesh=torus,
        in_specs=(
            P(REP, None, None, "tp"),
            P(None, REP, "tp"),
            P(None, REP, "tp"),
            P(REP, None, None, "tp"),
            P(None, REP, "tp"),
            P(None, REP, "tp"),
            P(REP, None, "tp", None),
            P(None, "tp", REP),
            P(None, "tp", REP),
        ),
        out_specs=(
            P(None, None, "tp"),
            P(None, REP, "tp"),
            P(None, REP, "tp"),
            P(None, None, "tp"),
            P(None, REP, "tp"),
            P(None, REP, "tp"),
            P(None, "tp", None),
            P(None, "tp", REP),
            P(None, "tp", REP),
        ),
        check_vma=False,
    )
```

profile of v0, /device:TPU:1, one launch (start us, length us, event | category | flops | bytes accessed | tf_op | source)
XLA Modules:
  0.0 191.4 jit_solution(4195767868516132089)
XLA Ops:
  7.2 0.0 copy-start.3
  7.2 6.2 %copy.70 = bf16[1,2,256,2048]{2,1,0,3:T(2,128)(2,1)} copy(bf16[1,2,256,2048]{3,2,1,0:T(8,128)(2,1)} %param.15) | data formatting | bytes 4194304 | tf_op args[6]
  13.4 0.0 copy-start.4
  13.4 9.6 %all-to-all-start.4 = ((bf16[1,2,256,2048]{2,1,0,3:T(2,128)(2,1)}), bf16[1,2,256,2048]{2,1,0,3:T(2,128)(2,1)S(1)}, u32[]{:S(2)}, u32[]{:S(2)}) async-start(bf16[1,2,256,2048]{2,1,0,3:T(2,128)(2,1)} %copy.70), calls=%async_computation.4 | async-start | bytes 4194304 | tf_op jit(solution)/shard_map/all_to_all | solution.py:71
  23.0 0.0 all-gather.5.cloned.1.call-start
  23.0 0.0 copy-done.3
  23.0 0.1 copy.71
  23.2 0.0 copy-done.4
  23.2 0.1 copy.72
  23.3 28.0 %all-to-all-done.4 = bf16[1,2,256,2048]{2,1,0,3:T(2,128)(2,1)S(1)} async-done(((bf16[1,2,256,2048]{2,1,0,3:T(2,128)(2,1)}), bf16[1,2,256,2048]{2,1,0,3:T(2,128)(2,1)S(1)}, u32[]{:S(2)}, u32[]{:S(2)}) %all-to-all-start.4) | async-done | bytes 2097184 | tf_op jit(solution)/shard_map/all_to_all | solution.py:71
  51.3 1.8 convert_reduce_fusion.1
  53.1 1.1 fusion
  54.2 0.0 all-gather.5.cloned.1.call-update
  54.2 0.0 all-gather.3.cloned.1.call-start
  54.2 2.4 %copy.65 = bf16[8,2,1,2,128,384]{5,4,0,3,2,1:T(8,128)(2,1)S(1)} copy(bf16[8,2,1,2,128,384]{5,4,1,0,3,2:T(8,128)(2,1)} %bitcast.14) | data formatting | bytes 6291456 | tf_op jit(solution)/shard_map/reshape | solution.py:26
  56.6 6.9 %all_to_all.33 = bf16[8,2,1,2,128,384]{5,4,0,3,2,1:T(8,128)(2,1)S(1)} all-to-all(bf16[8,2,1,2,128,384]{5,4,0,3,2,1:T(8,128)(2,1)S(1)} %copy.65), channel_id=1, replica_groups=mesh['rep_0'=2,'rep_1'=4,'rep_2'=2,'tp'=8] {'rep_2'}, dimensions={1} | all-to-all | bytes 6291456 | tf_op jit(solution)/shard_map/all_to_all | solution.py:28
  63.6 0.5 copy.66
  64.1 49.1 %all_to_all.34 = bf16[8,2,1,2,128,384]{5,4,1,3,2,0:T(8,128)(2,1)S(1)} all-to-all(bf16[8,2,1,2,128,384]{5,4,1,3,2,0:T(8,128)(2,1)S(1)} %copy.66), channel_id=1, replica_groups=mesh['rep_0'=2,'rep_1'=4,'rep_2'=2,'tp'=8] {'rep_0','rep_1'}, dimensions={0} | all-to-all | bytes 6291456 | tf_op jit(solution)/shard_map/all_to_all | solution.py:28
  113.2 0.0 copy-start.1
  113.2 0.0 copy-start.2
  113.2 0.0 copy-start
  113.2 0.4 convert_reduce_fusion
  113.7 0.6 copy-done.1
  114.2 0.1 copy-done.2
  114.3 1.0 fusion.2
  115.4 0.0 copy-start.5
  115.4 0.0 copy-start.6
  115.4 0.0 all-gather.3.cloned.1.call-update
  115.4 0.0 copy-done
  115.4 1.1 copy.67
  116.5 23.9 %all_to_all.35 = bf16[1,2,512,512]{3,1,0,2:T(2,128)(2,1)S(1)} all-to-all(bf16[1,2,512,512]{3,1,0,2:T(2,128)(2,1)S(1)} %copy.67), channel_id=1, replica_groups=mesh['rep_0'=2,'rep_1'=4,'rep_2'=2,'tp'=8] {'rep_0','rep_1','rep_2'}, dimensions={2} | all-to-all | bytes 2097152 | tf_op jit(solution)/shard_map/all_to_all | solution.py:70
  140.4 0.9 convert_reduce_fusion.2
  141.3 0.0 copy-done.5
  141.3 0.0 copy-done.6
  141.3 0.8 fusion.1
  142.0 1.1 broadcast_in_dim.2
  143.1 4.7 %all-to-all-start.3 = ((bf16[16,2,32,512]{3,2,1,0:T(8,128)(2,1)}), bf16[16,2,32,512]{3,2,1,0:T(8,128)(2,1)S(1)}, u32[]{:S(2)}, u32[]{:S(2)}) async-start(bf16[16,2,32,512]{3,2,1,0:T(8,128)(2,1)} %broadcast_in_dim.2), calls=%async_computation.3 | async-start | bytes 2097152 | tf_op jit(solution)/shard_map/all_to_all | solution.py:40
  147.8 0.8 copy.74
  148.7 0.8 copy.75
  149.5 23.9 %all-to-all-done.3 = bf16[16,2,32,512]{3,2,1,0:T(8,128)(2,1)S(1)} async-done(((bf16[16,2,32,512]{3,2,1,0:T(8,128)(2,1)}), bf16[16,2,32,512]{3,2,1,0:T(8,128)(2,1)S(1)}, u32[]{:S(2)}, u32[]{:S(2)}) %all-to-all-start.3) | async-done | bytes 1048608 | tf_op jit(solution)/shard_map/all_to_all | solution.py:40
  173.4 1.0 copy.69
  174.5 0.0 all-gather.5.cloned.1.call-done
  174.5 6.2 %copy.73 = bf16[2,256,2048]{2,1,0:T(8,128)(2,1)} copy(bf16[2,256,2048]{1,0,2:T(2,128)(2,1)} %all-gather.5.cloned.1.call-done) | data formatting | bytes 4194304
  180.7 0.0 all-gather.3.cloned.1.call-done
  180.7 3.9 %copy.86 = bf16[2,2048,384]{2,1,0:T(8,128)(2,1)} copy(bf16[2,2048,384]{2,1,0:T(8,128)(2,1)} %all-gather.3.cloned.1.call-done) | data formatting | bytes 6291456
Async XLA Ops:
  7.2 15.8 %copy-start.3 = (f32[2,256,128]{2,1,0:T(8,128)S(1)}, f32[2,256,128]{2,1,0:T(8,128)}, u32[]{:S(2)}) copy-start(f32[2,256,128]{2,1,0:T(8,128)} %param.17) | copy-start | bytes 786436
  13.4 9.8 %copy-start.4 = (f32[2,256,128]{2,1,0:T(8,128)S(1)}, f32[2,256,128]{2,1,0:T(8,128)}, u32[]{:S(2)}) copy-start(f32[2,256,128]{2,1,0:T(8,128)} %param.16) | copy-start | bytes 786436
  13.4 37.9 %all-to-all-start.4 = ((bf16[1,2,256,2048]{2,1,0,3:T(2,128)(2,1)}), bf16[1,2,256,2048]{2,1,0,3:T(2,128)(2,1)S(1)}, u32[]{:S(2)}, u32[]{:S(2)}) async-start(bf16[1,2,256,2048]{2,1,0,3:T(2,128)(2,1)} %copy.70), calls=%async_computation.4 | async-start | bytes 4194304 | tf_op jit(solution)/shard_map/all_to_all | solution.py:71
  23.0 151.5 %all-gather.5.cloned.1.call-start = ((), (), s32[]{:S(2)}) async-start(), calls=%async_computation.6 | async-start | bytes 2228224 | tf_op jit(solution)/shard_map/all_gather | solution.py:84
  54.2 126.5 %all-gather.3.cloned.1.call-start = ((), (), s32[]{:S(2)}) async-start(), calls=%async_computation.5 | async-start | bytes 3342336 | tf_op jit(solution)/shard_map/all_gather | solution.py:82
  113.2 1.0 copy-start.1
  113.2 1.1 copy-start.2
  113.2 2.2 %copy-start = (bf16[1,2,512,512]{3,2,1,0:T(8,128)(2,1)S(1)}, bf16[1,2,512,512]{3,2,1,0:T(8,128)(2,1)}, u32[]{:S(2)}) copy-start(bf16[1,2,512,512]{3,2,1,0:T(8,128)(2,1)} %param.12) | copy-start | bytes 3145732
  115.4 25.9 %copy-start.5 = (f32[2,32,512]{2,1,0:T(8,128)S(1)}, f32[2,32,512]{2,1,0:T(8,128)}, u32[]{:S(2)}) copy-start(f32[2,32,512]{2,1,0:T(8,128)} %param.13) | copy-start | bytes 393220
  115.4 25.9 %copy-start.6 = (f32[2,32,512]{2,1,0:T(8,128)S(1)}, f32[2,32,512]{2,1,0:T(8,128)}, u32[]{:S(2)}) copy-start(f32[2,32,512]{2,1,0:T(8,128)} %param.14) | copy-start | bytes 393220
  143.1 30.3 %all-to-all-start.3 = ((bf16[16,2,32,512]{3,2,1,0:T(8,128)(2,1)}), bf16[16,2,32,512]{3,2,1,0:T(8,128)(2,1)S(1)}, u32[]{:S(2)}, u32[]{:S(2)}) async-start(bf16[16,2,32,512]{3,2,1,0:T(8,128)(2,1)} %broadcast_in_dim.2), calls=%async_computation.3 | async-start | bytes 2097152 | tf_op jit(solution)/shard_map/all_to_all | solution.py:40
Sparse Core Ops, SparseCore 0:
  54.3 58.2 all-gather.4
  115.7 63.2 all-gather.2
where the time goes:
time: 192 us; the launch traced here: 191 us
  blocking collectives  79.9 us (42%)
  waiting for transfers between devices  51.9 us (27%)
  local copies, waits for them, and re-layouts  25 us (13%)
  starting transfers between devices  14.4 us (8%)
  between operations  14.2 us (7%)
  other arithmetic  5.96 us (3%)
    all_to_all x2, blocking collectives, moved_by_axis(): out = lax.all_to_all(out, axes[k], k, k, tiled=True)  56.1 us
    all_to_all x1, waiting for transfers between devices, outer_step(): lax.all_to_all(delta_output, REP, split_axis=3, concat_axis=0, tiled=True)  28 us
    all_to_all x1, waiting for transfers between devices, copy_for_each(): lax.all_to_all(jnp.broadcast_to(value[None], (length, *value.shape)), axi...  23.9 us
    all_to_all x1, blocking collectives, outer_step(): lax.all_to_all(delta_latent, REP, split_axis=2, concat_axis=0, tiled=True)  23.9 us
    unnamed x22, local copies, waits for them, and re-layouts  20 us
    all_to_all x1, starting transfers between devices, outer_step(): lax.all_to_all(delta_output, REP, split_axis=3, concat_axis=0, tiled=True)  9.58 us
    all_to_all x1, starting transfers between devices, copy_for_each(): lax.all_to_all(jnp.broadcast_to(value[None], (length, *value.shape)), axi...  4.7 us
  transfers between devices with their start and end apart: 4, of which 2 were waited for; matrix products, arithmetic and copies ran while one was open for 9% of the time, Pallas kernels for 0%

commit v1 on v0

--- a/solution.py
+++ b/solution.py
@@ -67,7 +67,10 @@
 ):
     replica_count = lax.axis_size(REP)
     query_terms = core_and_chips(delta_query, (("rep_0", "rep_1"), "rep_2"), (1, 0), 2, 0)
-    latent_terms = lax.all_to_all(delta_latent, REP, split_axis=2, concat_axis=0, tiled=True)
+    latent_terms = jnp.concatenate(
+        lax.all_to_all(jnp.stack(jnp.split(delta_latent, lax.axis_size(REP), axis=2)), REP, 0, 0),
+        axis=0,
+    )
     output_terms = lax.all_to_all(delta_output, REP, split_axis=3, concat_axis=0, tiled=True)
     query_totals = jnp.sum(query_terms.astype(jnp.float32), 0)
     latent_totals = jnp.sum(latent_terms.astype(jnp.float32), 0)

time: 192 us -> 190 us (0.990)
    unnamed x22 -> x36, local copies, waits for them, and re-layouts: 20 us -> 19 us
  transfers between devices with their start and end apart: 4 -> 4, of which waited for: 2 -> 2; matrix products, arithmetic and copies ran while one was open for 9% -> 8% of each run, Pallas kernels for 0% -> 0%
where the time goes in v1:
time: 190 us; the launch traced here: 189 us
  blocking collectives  79.9 us (42%)
  waiting for transfers between devices  51.3 us (27%)
  local copies, waits for them, and re-layouts  24 us (13%)
  starting transfers between devices  14.4 us (8%)
  between operations  14.3 us (8%)
  other arithmetic  5.21 us (3%)
    all_to_all x2, blocking collectives, moved_by_axis(): out = lax.all_to_all(out, axes[k], k, k, tiled=True)  56.1 us
    all_to_all x1, waiting for transfers between devices, outer_step(): lax.all_to_all(delta_output, REP, split_axis=3, concat_axis=0, tiled=True)  28 us
    all_to_all x1, blocking collectives, outer_step(): lax.all_to_all(jnp.stack(jnp.split(delta_latent, lax.axis_size(REP), axis...  23.9 us
    all_to_all x1, waiting for transfers between devices, copy_for_each(): lax.all_to_all(jnp.broadcast_to(value[None], (length, *value.shape)), axi...  23.3 us
    unnamed x36, local copies, waits for them, and re-layouts  19 us
    all_to_all x1, starting transfers between devices, outer_step(): lax.all_to_all(delta_output, REP, split_axis=3, concat_axis=0, tiled=True)  9.58 us
    all_to_all x1, starting transfers between devices, copy_for_each(): lax.all_to_all(jnp.broadcast_to(value[None], (length, *value.shape)), axi...  4.7 us
  transfers between devices with their start and end apart: 4, of which 2 were waited for; matrix products, arithmetic and copies ran while one was open for 8% of the time, Pallas kernels for 0%

profile of v1, /device:TPU:1, one launch (start us, length us, event | category | flops | bytes accessed | tf_op | source)
XLA Modules:
  0.0 189.1 jit_solution(3880137504730245485)
XLA Ops:
  7.2 0.0 copy-start.3
  7.2 6.2 %copy.43 = bf16[1,2,256,2048]{2,1,0,3:T(2,128)(2,1)} copy(bf16[1,2,256,2048]{3,2,1,0:T(8,128)(2,1)} %param.15) | data formatting | bytes 4194304 | tf_op args[6]
  13.4 0.0 copy-start.4
  13.4 9.6 %all-to-all-start.4 = ((bf16[1,2,256,2048]{2,1,0,3:T(2,128)(2,1)}), bf16[1,2,256,2048]{2,1,0,3:T(2,128)(2,1)S(1)}, u32[]{:S(2)}, u32[]{:S(2)}) async-start(bf16[1,2,256,2048]{2,1,0,3:T(2,128)(2,1)} %copy.43), calls=%async_computation.4 | async-start | bytes 4194304 | tf_op jit(solution)/shard_map/all_to_all | solution.py:74
  23.0 0.0 all-gather.5.cloned.1.call-start
  23.0 0.0 copy-done.3
  23.0 0.1 copy.44
  23.2 0.0 copy-done.4
  23.2 0.1 copy.45
  23.3 28.0 %all-to-all-done.4 = bf16[1,2,256,2048]{2,1,0,3:T(2,128)(2,1)S(1)} async-done(((bf16[1,2,256,2048]{2,1,0,3:T(2,128)(2,1)}), bf16[1,2,256,2048]{2,1,0,3:T(2,128)(2,1)S(1)}, u32[]{:S(2)}, u32[]{:S(2)}) %all-to-all-start.4) | async-done | bytes 2097184 | tf_op jit(solution)/shard_map/all_to_all | solution.py:74
  51.3 1.8 convert_reduce_fusion.1
  53.1 1.1 fusion
  54.2 0.0 all-gather.5.cloned.1.call-update
  54.2 0.0 all-gather.3.cloned.1.call-start
  54.2 2.4 %copy.40 = bf16[8,2,1,2,128,384]{5,4,0,3,2,1:T(8,128)(2,1)S(1)} copy(bf16[8,2,1,2,128,384]{5,4,1,0,3,2:T(8,128)(2,1)} %bitcast.43) | data formatting | bytes 6291456 | tf_op jit(solution)/shard_map/reshape | solution.py:26
  56.6 6.9 %all_to_all.29 = bf16[8,2,1,2,128,384]{5,4,0,3,2,1:T(8,128)(2,1)S(1)} all-to-all(bf16[8,2,1,2,128,384]{5,4,0,3,2,1:T(8,128)(2,1)S(1)} %copy.40), channel_id=1, replica_groups=mesh['rep_0'=2,'rep_1'=4,'rep_2'=2,'tp'=8] {'rep_2'}, dimensions={1} | all-to-all | bytes 6291456 | tf_op jit(solution)/shard_map/all_to_all | solution.py:28
  63.6 0.5 copy.41
  64.1 49.1 %all_to_all.30 = bf16[8,2,1,2,128,384]{5,4,1,3,2,0:T(8,128)(2,1)S(1)} all-to-all(bf16[8,2,1,2,128,384]{5,4,1,3,2,0:T(8,128)(2,1)S(1)} %copy.41), channel_id=1, replica_groups=mesh['rep_0'=2,'rep_1'=4,'rep_2'=2,'tp'=8] {'rep_0','rep_1'}, dimensions={0} | all-to-all | bytes 6291456 | tf_op jit(solution)/shard_map/all_to_all | solution.py:28
  113.2 0.0 copy-start.1
  113.2 0.0 copy-start.2
  113.2 0.0 copy-start
  113.2 0.4 convert_reduce_fusion
  113.7 0.6 copy-done.1
  114.2 0.1 copy-done.2
  114.3 1.0 fusion.2
  115.4 0.0 copy-start.5
  115.4 0.0 copy-start.6
  115.4 0.0 all-gather.3.cloned.1.call-update
  115.4 0.0 copy-done
  115.7 23.9 %all_to_all.31 = bf16[16,1,2,32,512]{4,3,2,1,0:T(8,128)(2,1)S(1)} all-to-all(bf16[16,1,2,32,512]{4,3,2,1,0:T(8,128)(2,1)S(1)} %bitcast_dynamic-update-slice_fusion), channel_id=1, replica_groups=mesh['rep_0'=2,'rep_1'=4,'rep_2'=2,'tp'=8] {'rep_0','rep_1','rep_2'}, dimensions={0} | all-to-all | bytes 2097152 | tf_op jit(solution)/shard_map/all_to_all | solution.py:71
  139.5 0.1 convert_reduce_fusion.2
  139.7 0.0 copy-done.5
  139.7 0.0 copy-done.6
  139.7 0.7 fusion.1
  140.4 1.1 broadcast_in_dim.2
  141.5 4.7 %all-to-all-start.3 = ((bf16[16,2,32,512]{3,2,1,0:T(8,128)(2,1)}), bf16[16,2,32,512]{3,2,1,0:T(8,128)(2,1)S(1)}, u32[]{:S(2)}, u32[]{:S(2)}) async-start(bf16[16,2,32,512]{3,2,1,0:T(8,128)(2,1)} %broadcast_in_dim.2), calls=%async_computation.3 | async-start | bytes 2097152 | tf_op jit(solution)/shard_map/all_to_all | solution.py:40
  146.2 0.8 copy.47
  147.1 0.8 copy.48
  147.9 23.3 %all-to-all-done.3 = bf16[16,2,32,512]{3,2,1,0:T(8,128)(2,1)S(1)} async-done(((bf16[16,2,32,512]{3,2,1,0:T(8,128)(2,1)}), bf16[16,2,32,512]{3,2,1,0:T(8,128)(2,1)S(1)}, u32[]{:S(2)}, u32[]{:S(2)}) %all-to-all-start.3) | async-done | bytes 1048608 | tf_op jit(solution)/shard_map/all_to_all | solution.py:40
  171.2 1.0 copy.42
  172.3 0.0 all-gather.5.cloned.1.call-done
  172.3 6.2 %copy.46 = bf16[2,256,2048]{2,1,0:T(8,128)(2,1)} copy(bf16[2,256,2048]{1,0,2:T(2,128)(2,1)} %all-gather.5.cloned.1.call-done) | data formatting | bytes 4194304
  178.4 0.0 all-gather.3.cloned.1.call-done
  178.4 3.9 %copy.67 = bf16[2,2048,384]{2,1,0:T(8,128)(2,1)} copy(bf16[2,2048,384]{2,1,0:T(8,128)(2,1)} %all-gather.3.cloned.1.call-done) | data formatting | bytes 6291456
  (16 shorter events, 0.1 us)
Async XLA Ops:
  7.2 15.8 %copy-start.3 = (f32[2,256,128]{2,1,0:T(8,128)S(1)}, f32[2,256,128]{2,1,0:T(8,128)}, u32[]{:S(2)}) copy-start(f32[2,256,128]{2,1,0:T(8,128)} %param.17) | copy-start | bytes 786436
  13.4 9.8 %copy-start.4 = (f32[2,256,128]{2,1,0:T(8,128)S(1)}, f32[2,256,128]{2,1,0:T(8,128)}, u32[]{:S(2)}) copy-start(f32[2,256,128]{2,1,0:T(8,128)} %param.16) | copy-start | bytes 786436
  13.4 37.9 %all-to-all-start.4 = ((bf16[1,2,256,2048]{2,1,0,3:T(2,128)(2,1)}), bf16[1,2,256,2048]{2,1,0,3:T(2,128)(2,1)S(1)}, u32[]{:S(2)}, u32[]{:S(2)}) async-start(bf16[1,2,256,2048]{2,1,0,3:T(2,128)(2,1)} %copy.43), calls=%async_computation.4 | async-start | bytes 4194304 | tf_op jit(solution)/shard_map/all_to_all | solution.py:74
  23.0 149.3 %all-gather.5.cloned.1.call-start = ((), (), s32[]{:S(2)}) async-start(), calls=%async_computation.6 | async-start | bytes 2228224 | tf_op jit(solution)/shard_map/all_gather | solution.py:87
  54.2 124.2 %all-gather.3.cloned.1.call-start = ((), (), s32[]{:S(2)}) async-start(), calls=%async_computation.5 | async-start | bytes 3342336 | tf_op jit(solution)/shard_map/all_gather | solution.py:85
  113.2 1.0 copy-start.1
  113.2 1.1 copy-start.2
  113.2 2.2 %copy-start = (bf16[1,2,512,512]{3,2,1,0:T(8,128)(2,1)S(1)}, bf16[1,2,512,512]{3,2,1,0:T(8,128)(2,1)}, u32[]{:S(2)}) copy-start(bf16[1,2,512,512]{3,2,1,0:T(8,128)(2,1)} %param.12) | copy-start | bytes 3145732
  115.4 24.3 %copy-start.5 = (f32[2,32,512]{2,1,0:T(8,128)S(1)}, f32[2,32,512]{2,1,0:T(8,128)}, u32[]{:S(2)}) copy-start(f32[2,32,512]{2,1,0:T(8,128)} %param.13) | copy-start | bytes 393220
  115.4 24.3 %copy-start.6 = (f32[2,32,512]{2,1,0:T(8,128)S(1)}, f32[2,32,512]{2,1,0:T(8,128)}, u32[]{:S(2)}) copy-start(f32[2,32,512]{2,1,0:T(8,128)} %param.14) | copy-start | bytes 393220
  141.5 29.7 %all-to-all-start.3 = ((bf16[16,2,32,512]{3,2,1,0:T(8,128)(2,1)}), bf16[16,2,32,512]{3,2,1,0:T(8,128)(2,1)S(1)}, u32[]{:S(2)}, u32[]{:S(2)}) async-start(bf16[16,2,32,512]{3,2,1,0:T(8,128)(2,1)} %broadcast_in_dim.2), calls=%async_computation.3 | async-start | bytes 2097152 | tf_op jit(solution)/shard_map/all_to_all | solution.py:40
Sparse Core Ops, SparseCore 0:
  54.3 58.2 all-gather.4
  115.7 62.1 all-gather.2
